TPU v7x, 32 devices: a whole 2x2x4 slice. The times are simulated.
32 devices in a mesh: blk: 8 (over y, x, core), grp: 4 (over z).
Axes of the slice: x: 2, y: 2, z: 4, core: 2. Of those that a mesh axis runs over, the one named last changes fastest.
Arguments:
- samples: float32 [32, 128, 256], P('blk', 'grp'), may hold values from -11 to 11
- pair_table: int32 [32, 16], P('blk'), may hold values from 0 to 31
- assignment: int32 [2, 32], P(None, 'blk'), may hold values from 0 to 127
- band_index: int32 [2], replicated, may hold values from 0 to 1023
Outputs:
- log_weight: float32 [2, 32, 128], P(None, 'blk', 'grp')
All inputs are finite; a program needn't handle non-finite values.
Results may differ from a plain program's by a relative error of at most 0.0003.
Values sent between devices are 32-bit elements; how exact they have to be, the bound alone decides.
No kernel may reach another device: no remote copies, remote signals or barrier semaphores. Data moves between devices by JAX's collectives and lax.ppermute only.
A program may use at most 128 MiB of HBM per device.

v0:
```python
import functools

import jax
import jax.numpy as jnp
from jax import lax
from jax.experimental import pallas as pl
from jax.experimental.pallas import tpu as pltpu
from jax.sharding import PartitionSpec as P


HIGH = lax.Precision.HIGHEST
NN = (((1,), (0,)), ((), ()))
LOG2E = 1.4426950408889634
LEFT = (0, 0, 1, 1, 0, 2)
RIGHT = (0, 1, 0, 1, 2, 0)


def split(value):
    first = value.astype(jnp.bfloat16)
    rest = value - first.astype(jnp.float32)
    second = rest.astype(jnp.bfloat16)
    third = (rest - second.astype(jnp.float32)).astype(jnp.bfloat16)
    return first, second, third


def fill(stack, at, value, order, axis):
    parts = split(value)
    for i, k in enumerate(order):
        size = value.shape[axis]
        if axis:
            stack[at : at + value.shape[0], i * size : (i + 1) * size] = parts[k]
        else:
            stack[i * size : (i + 1) * size, at : at + value.shape[1]] = parts[k]


def prepare_kernel(first_ref, assign_hbm, x_hbm, out_ref, assign_ref, sems, *, subs, rows, rounds):
    lanes = subs * rows
    assign = pltpu.make_async_copy(assign_hbm, assign_ref, sems.at[0])
    assign.start()
    load = pltpu.make_async_copy(x_hbm, out_ref.at[pl.ds(0, lanes)], sems.at[1])
    load.start()
    lane = lax.broadcasted_iota(jnp.int32, (8, lanes), 1)
    line = lax.broadcasted_iota(jnp.int32, (8, lanes), 0)
    own = lane % rows + first_ref[...]
    assign.wait()
    weight = jnp.zeros((8, lanes), jnp.float32)
    for turn in range(rounds):
        for sub in range(subs):
            mine = (line == turn) & (lane // rows == sub)
            chosen = assign_ref[turn : turn + 1, sub : sub + 1]
            weight = jnp.where(mine & (own == chosen), 1.0, weight)
    load.wait()
    out_ref[lanes:, :] = lax.dot_general(
        weight, out_ref[:lanes, :], NN, precision=HIGH, preferred_element_type=jnp.float32
    )


def layout(groups, rounds, pairs, width, lanes):
    cross = groups * rounds * pairs
    norm = cross + groups * rounds
    centre = norm + groups
    height = centre + rounds * (width // lanes)
    return cross, norm, centre, -(-height // 8) * 8


def wide(row, count):
    return jnp.concatenate([row] * (count // row.shape[1]), 1)


def take_queries(refs, lanes, terms, norm):
    for i, ref in enumerate(refs):
        q = ref[:lanes, :].T
        here = slice(i * lanes, (i + 1) * lanes)
        norm[:, here] = jnp.broadcast_to(jnp.sum(q * q, 0, keepdims=True), (8, lanes))
        fill(terms, i * lanes, -2.0 * q, RIGHT, 0)


def take_keys(refs, lanes, stack):
    for i, ref in enumerate(refs):
        fill(stack, i * lanes, ref[:lanes, :], LEFT, 1)


def scan(
    inverse_ref, refs, stack, terms, low, totals, *, first, columns, subs, rows, rounds
):
    lanes = subs * rows
    count = terms.shape[1]
    part = lax.dot_general(stack[...], terms[...], NN, preferred_element_type=jnp.float32)
    inverse = [wide(LOG2E * inverse_ref[t : t + 1, :], count) for t in range(rounds)]
    for i, ref in enumerate(refs):
        keys = ref[:lanes, :]
        norm = jnp.sum(keys * keys, -1, keepdims=True)
        for sub in range(subs):
            mine = slice(sub * rows, (sub + 1) * rows)
            tile = part[i * lanes + sub * rows : i * lanes + (sub + 1) * rows] + norm[mine]
            smallest = jnp.min(tile, 0, keepdims=True)
            gap = smallest - tile
            at = (first + i) * subs + sub
            low[at : at + 1, columns] = smallest
            for turn in range(rounds):
                totals[turn, at : at + 1, columns] = jnp.sum(
                    jnp.exp2(gap * inverse[turn]), 0, keepdims=True
                )


def early_kernel(inverse_ref, *refs, near, chunks, subs, rows, rounds):
    lanes = subs * rows
    key_refs = refs[:near]
    query_refs = refs[near : near + chunks]
    terms, norm, stack, low, totals = refs[near + chunks :]
    take_queries(query_refs, lanes, terms, norm)
    take_keys(key_refs, lanes, stack)
    scan(
        inverse_ref,
        key_refs,
        stack,
        terms,
        low,
        totals,
        first=0,
        columns=slice(None),
        subs=subs,
        rows=rows,
        rounds=rounds,
    )


def score_kernel(
    inverse_ref,
    hot_ref,
    near_terms,
    near_norm,
    near_stack,
    near_low,
    near_totals,
    *refs,
    chunks,
    later,
    near,
    blocks,
    groups,
    subs,
    rows,
    rounds,
    pairs,
    members,
):
    key_refs = refs[:blocks]
    query_refs = refs[blocks : blocks + len(later)]
    out_ref, terms, norm, stack, low, totals = refs[blocks + len(later) :]
    lanes = subs * rows
    width = key_refs[0].shape[1]
    before = len(chunks) * lanes
    count = before + len(later) * lanes
    cross_at, norm_at, centre_at, _ = layout(groups, rounds, pairs, width, lanes)
    sizes = {"subs": subs, "rows": rows, "rounds": rounds}
    old, new = slice(0, before), slice(before, count)
    take_keys(key_refs[near:], lanes, stack)
    scan(
        inverse_ref, key_refs[near:], stack, near_terms, low, totals, first=near, columns=old, **sizes
    )
    take_queries(query_refs, lanes, terms, norm)
    scan(
        inverse_ref, key_refs[:near], near_stack, terms, low, totals, first=0, columns=new, **sizes
    )
    scan(
        inverse_ref, key_refs[near:], stack, terms, low, totals, first=near, columns=new, **sizes
    )
    done = near * subs
    low[:done, old] = near_low[...]
    totals[:, :done, old] = near_totals[...]
    centre = sum(ref[lanes:, :] for ref in key_refs) / members
    a = split(centre)
    left = jnp.concatenate([a[k] for k in LEFT], 1)
    cross = jnp.concatenate(
        [
            lax.dot_general(left, right[...], NN, preferred_element_type=jnp.float32)
            for right in (near_terms, terms)
        ],
        1,
    )
    query_norm = jnp.concatenate([near_norm[:1, :], norm[:1, :]], 1)
    nearest = low[...] + query_norm
    hot = hot_ref[...]
    lane = lax.broadcasted_iota(jnp.int32, (pairs, lanes), 1) // rows
    every = tuple(chunks) + tuple(later)
    for turn in range(rounds):
        value = jnp.log(totals[turn]) - nearest * wide(inverse_ref[turn : turn + 1, :], count)
        chosen = lax.dot_general(
            hot, value, NN, precision=HIGH, preferred_element_type=jnp.float32
        )
        for i, k in enumerate(every):
            piece = chosen[:, i * lanes : (i + 1) * lanes]
            merged = piece[:pairs]
            for sub in range(1, subs):
                merged = jnp.where(lane == sub, piece[sub * pairs : (sub + 1) * pairs], merged)
            at = (k * rounds + turn) * pairs
            out_ref[at : at + pairs, :] = merged
    for i, k in enumerate(every):
        out_ref[cross_at + k * rounds : cross_at + (k + 1) * rounds, :] = cross[
            :rounds, i * lanes : (i + 1) * lanes
        ]
        out_ref[norm_at + k : norm_at + k + 1, :] = query_norm[:, i * lanes : (i + 1) * lanes]
    for turn in range(rounds):
        for c in range(width // lanes):
            at = centre_at + turn * (width // lanes) + c
            out_ref[at : at + 1, :] = centre[turn : turn + 1, c * lanes : (c + 1) * lanes]


def finish_kernel(inverse_ref, *refs, groups, subs, rows, rounds, pairs, width):
    parts = refs[:groups]
    out_ref = refs[groups]
    lanes = subs * rows
    cross_at, norm_at, centre_at, _ = layout(groups, rounds, pairs, width, lanes)
    step = rounds * pairs
    sums = []
    cross = []
    for k in range(groups):
        pieces = [parts[j][(k ^ j) * step : ((k ^ j) + 1) * step, :] for j in range(groups)]
        peak = functools.reduce(jnp.maximum, pieces)
        total = sum(jnp.exp(piece - peak) for piece in pieces)
        sums.append(peak + jnp.log(total))
        at = [cross_at + (k ^ j) * rounds for j in range(groups)]
        cross.append(sum(parts[j][at[j] : at[j] + rounds, :] for j in range(groups)))
    kernel = jnp.concatenate(sums, 0).reshape(groups * rounds, pairs, lanes)
    weighted = jnp.sum(kernel, 1) / pairs
    cross = jnp.concatenate(cross, 0)
    halves = width // lanes
    centre = sum(part[centre_at : centre_at + rounds * halves, :] for part in parts)
    centre_sq = jnp.sum(centre * centre, -1, keepdims=True)
    group_of = lax.broadcasted_iota(jnp.int32, (1, lanes), 1) // rows
    line = lax.broadcasted_iota(jnp.int32, (groups * rounds, lanes), 0)
    inverse = jnp.zeros((groups * rounds, lanes), jnp.float32)
    constant = jnp.zeros((groups * rounds, lanes), jnp.float32)
    norm = jnp.zeros((groups * rounds, lanes), jnp.float32)
    for turn in range(rounds):
        mine = line % rounds == turn
        inverse = jnp.where(mine, inverse_ref[turn : turn + 1, :], inverse)
        square = sum(
            centre_sq[turn * halves + c : turn * halves + c + 1, :] for c in range(halves)
        )
        constant = jnp.where(mine, square, constant)
    for k in range(groups):
        norm = jnp.where(line // rounds == k, parts[0][norm_at + k : norm_at + k + 1, :], norm)
    logits = weighted - (norm + cross + constant) * inverse

    def over_draws(value, combine, reduce, neutral):
        shift = rounds
        while shift < groups * rounds:
            value = combine(value, pltpu.roll(value, shift, 0))
            shift *= 2
        result = value
        for sub in range(subs):
            here = reduce(jnp.where(group_of == sub, value, neutral), -1, keepdims=True)
            result = jnp.where(group_of == sub, here, result)
        return result

    peak = over_draws(logits, jnp.maximum, jnp.max, -jnp.inf)
    shifted = logits - peak
    total = over_draws(jnp.exp(shifted), jnp.add, jnp.sum, 0.0)
    value = shifted - jnp.log(total)
    for turn in range(rounds):
        for sub in range(subs):
            out_ref[turn, sub : sub + 1, :] = value[
                turn : turn + 1, sub * rows : (sub + 1) * rows
            ]


def program(samples, pair_table, assignment, band_index):
    subs, rows, width = samples.shape
    rounds = assignment.shape[0]
    pairs = pair_table.shape[1]
    groups = lax.axis_size("grp")
    blocks = lax.axis_size("blk")
    members = subs * blocks
    lanes = subs * rows
    group = lax.axis_index("grp")
    block = lax.axis_index("blk")

    def over(axis, size, value, k):
        return lax.ppermute(value, axis, [(i, i ^ k) for i in range(size)])

    vmem = pl.BlockSpec(memory_space=pltpu.VMEM)
    hbm = pl.BlockSpec(memory_space=pl.ANY)

    def call(kernel, shapes, arrays, scratch=(), **sizes):
        one = not isinstance(shapes, list)
        outs = [
            jax.ShapeDtypeStruct(shape[:-1], shape[-1])
            for shape in ([shapes] if one else shapes)
        ]
        return pl.pallas_call(
            functools.partial(kernel, **sizes),
            out_shape=outs[0] if one else outs,
            in_specs=[vmem] * len(arrays),
            out_specs=vmem if one else [vmem] * len(outs),
            scratch_shapes=[pltpu.VMEM(shape[:-1], shape[-1]) for shape in scratch],
            compiler_params=pltpu.CompilerParams(
                vmem_limit_bytes=(16 if blocks <= 8 else 48) * 2**20
            ),
        )(*arrays)

    f32, bf16 = jnp.float32, jnp.bfloat16
    x = samples.reshape(lanes, width)
    queries = {k: over("grp", groups, x, k) for k in range(groups - 1, 0, -1)}
    own = pl.pallas_call(
        functools.partial(prepare_kernel, subs=subs, rows=rows, rounds=rounds),
        out_shape=jax.ShapeDtypeStruct((lanes + 8, width), f32),
        in_specs=[vmem, hbm, hbm],
        out_specs=vmem,
        scratch_shapes=[
            pltpu.VMEM((rounds, subs), jnp.int32),
            pltpu.SemaphoreType.DMA((2,)),
        ],
        compiler_params=pltpu.CompilerParams(vmem_limit_bytes=4 * 2**20),
        name="prepare",
    )(jnp.full((1, lanes), group * rows, jnp.int32), assignment, x)
    keys = {0: own}
    for k in range(2, blocks, 2):
        keys[k] = over("blk", blocks, own, k)
    for k in range(0, blocks, 2):
        keys[k ^ 1] = over("blk", blocks, keys[k], 1)
    queries[0] = own
    place = (pair_table // subs ^ block) * subs + pair_table % subs
    hot = (
        place.reshape(subs * pairs, 1) == jnp.arange(members, dtype=jnp.int32)[None, :]
    ).astype(f32)
    band_sq = width * (1.0 + band_index.astype(f32) / 256.0) / 32.0
    inverse = jnp.broadcast_to((1.0 / (2.0 * band_sq))[:, None], (rounds, lanes))
    height = layout(groups, rounds, pairs, width, lanes)[-1]
    order = CHUNKS if groups == len(CHUNKS) else tuple(range(groups))
    chunks, later = order[: groups // 2], order[groups // 2 :]
    near = blocks // 2
    before, after = len(chunks) * lanes, len(later) * lanes
    sizes = {"subs": subs, "rows": rows, "rounds": rounds}
    known = call(
        early_kernel,
        [
            (len(RIGHT) * width, before, bf16),
            (8, before, f32),
            (near * lanes, len(LEFT) * width, bf16),
            (near * subs, before, f32),
            (rounds, near * subs, before, f32),
        ],
        [inverse] + [keys[k] for k in range(near)] + [queries[k] for k in chunks],
        near=near,
        chunks=len(chunks),
        **sizes,
    )
    part = call(
        score_kernel,
        (height, lanes, f32),
        [inverse, hot, *known]
        + [keys[k] for k in range(blocks)]
        + [queries[k] for k in later],
        scratch=[
            (len(RIGHT) * width, after, bf16),
            (8, after, f32),
            ((blocks - near) * lanes, len(LEFT) * width, bf16),
            (members, before + after, f32),
            (rounds, members, before + after, f32),
        ],
        chunks=chunks,
        later=later,
        near=near,
        blocks=blocks,
        groups=groups,
        pairs=pairs,
        members=members,
        **sizes,
    )
    parts = {k: over("grp", groups, part, k) for k in range(groups - 1, 0, -1)}
    parts[0] = part
    return call(
        finish_kernel,
        (rounds, subs, rows, f32),
        [inverse] + [parts[k] for k in range(groups)],
        groups=groups,
        pairs=pairs,
        width=width,
        **sizes,
    )


CHUNKS = (0, 2, 3, 1)


def solution(mesh):
    return jax.shard_map(
        program,
        mesh=mesh,
        in_specs=(P("blk", "grp", None), P("blk", None), P(None, "blk"), P()),
        out_specs=P(None, "blk", "grp"),
        check_vma=False,
    )
```

profile of v0, /device:TPU:0, one launch (start us, length us, event | category | flops | bytes accessed | tf_op | source)
XLA Modules:
  0.0 37.8 jit_solution(13469205028426665067)
XLA Ops:
  0.0 0.7 %copy-done = s32[2,4]{1,0:T(2,128)S(1)} copy-done((s32[2,4]{1,0:T(2,128)S(1)}, s32[2,4]{1,0:T(2,128)}, u32[]{:S(2)}) %copy-start) | copy-done | bytes 56
  0.7 1.1 %prepare.1.refs_0_.refs_4_ = f32[136,256]{1,0:T(8,128)S(1)} custom-call(s32[1,128]{1,0:T(1,128)S(1)} %broadcast_in_dim.5.first_ref, s32[2,4]{1,0:T(2,128)S(1)} %copy-done, f32[128,256]{1,0:T(8,128)} %bitcast.x_hbm), custom_call_target="tpu_custom_call" | custom-call | tf_op jit(solution)/shard_map/prepare/pallas_call | solution.py:306
  1.8 3.0 %collective-permute-start.1 = (f32[136,256]{1,0:T(8,128)S(1)}, f32[136,256]{1,0:T(8,128)S(1)}, u32[]{:S(2)}, u32[]{:S(2)}) collective-permute-start(f32[136,256]{1,0:T(8,128)S(1)} %prepare.1.refs_0_.refs_4_), channel_id=1, source_target_pairs={{0,8},{4,12},{8,0},{12,4},{16,24},{20,28},{24,16},{28,20},{1,9},{5... | collective-permute-start | bytes 417800 | tf_op jit(solution)/shard_map/ppermute | solution.py:281
  4.8 2.6 %collective-permute-start.3 = (f32[128,256]{1,0:T(8,128)}, f32[128,256]{1,0:T(8,128)S(1)}, u32[]{:S(2)}, u32[]{:S(2)}) collective-permute-start(f32[128,256]{1,0:T(8,128)} %bitcast.x_hbm), channel_id=1, source_target_pairs={{0,2},{1,3},{2,0},{3,1},{4,6},{5,7},{6,4},{7,5},{8,10},{9,11},{10,... | collective-permute-start | bytes 393224 | tf_op jit(solution)/shard_map/ppermute | solution.py:281
  7.4 1.5 %collective-permute-start.4 = (f32[136,256]{1,0:T(8,128)S(1)}, f32[136,256]{1,0:T(8,128)S(1)}, u32[]{:S(2)}, u32[]{:S(2)}) collective-permute-start(f32[136,256]{1,0:T(8,128)S(1)} %prepare.1.refs_0_.refs_4_), channel_id=1, source_target_pairs={{0,16},{4,20},{8,24},{12,28},{16,0},{20,4},{24,8},{28,12},{1,17},{... | collective-permute-start | bytes 417800 | tf_op jit(solution)/shard_map/ppermute | solution.py:281
  8.9 0.5 %collective-permute-start.6 = (f32[136,256]{1,0:T(8,128)S(1)}, f32[136,256]{1,0:T(8,128)S(1)}, u32[]{:S(2)}, u32[]{:S(2)}) collective-permute-start(f32[136,256]{1,0:T(8,128)S(1)} %prepare.1.refs_0_.refs_4_), channel_id=1, source_target_pairs={{0,24},{4,28},{8,16},{12,20},{16,8},{20,12},{24,0},{28,4},{1,25},{... | collective-permute-start | bytes 417800 | tf_op jit(solution)/shard_map/ppermute | solution.py:281
  9.4 0.7 %fusion.3 = s32[4,16]{1,0:T(4,128)S(1)} fusion(s32[4,16]{1,0:T(4,128)} %param.5, s32[]{:T(128)S(6)} %axis_index.23), kind=kLoop, calls=%fused_computation.9 | loop fusion | flops 1408 | bytes 516 | tf_op jit(solution)/shard_map/add | solution.py:324
  10.1 0.1 eq.17
  10.3 4.4 %collective-permute-done.3.refs_5_ = f32[128,256]{1,0:T(8,128)S(1)} collective-permute-done((f32[128,256]{1,0:T(8,128)}, f32[128,256]{1,0:T(8,128)S(1)}, u32[]{:S(2)}, u32[]{:S(2)}) %collective-permute-start.3) | collective-permute-done | bytes 131104 | tf_op jit(solution)/shard_map/ppermute | solution.py:281
  14.6 3.5 %collective-permute-start.8 = (f32[128,256]{1,0:T(8,128)}, f32[128,256]{1,0:T(8,128)S(1)}, u32[]{:S(2)}, u32[]{:S(2)}) collective-permute-start(f32[128,256]{1,0:T(8,128)} %bitcast.x_hbm), channel_id=1, source_target_pairs={{0,3},{1,2},{2,1},{3,0},{4,7},{5,6},{6,5},{7,4},{8,11},{9,10},{10,... | collective-permute-start | bytes 393224 | tf_op jit(solution)/shard_map/ppermute | solution.py:281
  18.2 0.5 %collective-permute-start.5 = (f32[136,256]{1,0:T(8,128)S(1)}, f32[136,256]{1,0:T(8,128)S(1)}, u32[]{:S(2)}, u32[]{:S(2)}) collective-permute-start(f32[136,256]{1,0:T(8,128)S(1)} %collective-permute-done.4.refs_4_), channel_id=1, source_target_pairs={{0,4},{4,0},{8,12},{12,8},{16,20},{20,16},{24,28},{28,24},{1,5},{5... | collective-permute-start | bytes 417800 | tf_op jit(solution)/shard_map/ppermute | solution.py:281
  18.7 0.1 collective-permute-start.7
  18.8 0.7 %multiply_divide_fusion = f32[2]{0:T(128)S(1)} fusion(s32[2]{0:T(128)} %param.7), kind=kLoop, calls=%fused_computation.13 | loop fusion | flops 10 | bytes 16 | tf_op jit(solution)/shard_map/div | solution.py:329
  19.5 0.1 collective-permute-done.2.refs_3_
  19.6 1.0 %shard_map.46 = (bf16[1536,256]{1,0:T(8,128)(2,1)S(1)}, f32[8,256]{1,0:T(8,128)S(1)}, bf16[512,1536]{1,0:T(8,128)(2,1)S(1)}, f32[16,256]{1,0:T(8,128)S(1)}, f32[2,16,256]{2,1,0:T(8,128)S(1)}) custom-call(f32[2,128]{1,0:T(2,128)S(1)} %broadcast_in_dim.4.inverse_ref, f32[136,256]{1,0:T(8,128)S(1)} %prepare.1.refs_0_.refs_4_, ...), custom_call_target="tpu_custom_call" | custom-call | tf_op jit(solution)/shard_map/pallas_call | solution.py:292
  20.6 2.4 %collective-permute-done.8.refs_8_ = f32[128,256]{1,0:T(8,128)S(1)} collective-permute-done((f32[128,256]{1,0:T(8,128)}, f32[128,256]{1,0:T(8,128)S(1)}, u32[]{:S(2)}, u32[]{:S(2)}) %collective-permute-start.8) | collective-permute-done | bytes 131104 | tf_op jit(solution)/shard_map/ppermute | solution.py:281
  23.1 1.9 %collective-permute-done.9.refs_9_ = f32[128,256]{1,0:T(8,128)S(1)} collective-permute-done((f32[128,256]{1,0:T(8,128)}, f32[128,256]{1,0:T(8,128)S(1)}, u32[]{:S(2)}, u32[]{:S(2)}) %collective-permute-start.9) | collective-permute-done | bytes 131104 | tf_op jit(solution)/shard_map/ppermute | solution.py:281
  25.0 2.5 %shard_map.47.refs_0_ = f32[144,128]{1,0:T(8,128)S(1)} custom-call(f32[2,128]{1,0:T(2,128)S(1)} %broadcast_in_dim.4.inverse_ref, f32[64,32]{1,0:T(8,128)S(1)} %fusion.hot_ref, bf16[1536,256]{1,0:T(8,128)(2,1)S(1)} %get-tuple-element.10.near_terms, f32[8,256]{1,0:T(8,128)S(1)} %get-tuple-element.11.near_norm, ...), custom_call_target="tpu_custom_call" | custom-call | tf_op jit(solution)/shard_map/pallas_call | solution.py:292
  27.5 1.7 %collective-permute-start.10 = (f32[144,128]{1,0:T(8,128)S(1)}, f32[144,128]{1,0:T(8,128)S(1)}, u32[]{:S(2)}, u32[]{:S(2)}) collective-permute-start(f32[144,128]{1,0:T(8,128)S(1)} %shard_map.47.refs_0_), channel_id=1, source_target_pairs={{0,1},{1,0},{2,3},{3,2},{4,5},{5,4},{6,7},{7,6},{8,9},{9,8},{10,11... | collective-permute-start | bytes 221192 | tf_op jit(solution)/shard_map/ppermute | solution.py:281
  29.2 0.6 %collective-permute-start.11 = (f32[144,128]{1,0:T(8,128)S(1)}, f32[144,128]{1,0:T(8,128)S(1)}, u32[]{:S(2)}, u32[]{:S(2)}) collective-permute-start(f32[144,128]{1,0:T(8,128)S(1)} %shard_map.47.refs_0_), channel_id=1, source_target_pairs={{0,2},{1,3},{2,0},{3,1},{4,6},{5,7},{6,4},{7,5},{8,10},{9,11},{10,... | collective-permute-start | bytes 221192 | tf_op jit(solution)/shard_map/ppermute | solution.py:281
  29.8 2.2 %collective-permute-start.12 = (f32[144,128]{1,0:T(8,128)S(1)}, f32[144,128]{1,0:T(8,128)S(1)}, u32[]{:S(2)}, u32[]{:S(2)}) collective-permute-start(f32[144,128]{1,0:T(8,128)S(1)} %shard_map.47.refs_0_), channel_id=1, source_target_pairs={{0,3},{1,2},{2,1},{3,0},{4,7},{5,6},{6,5},{7,4},{8,11},{9,10},{10,... | collective-permute-start | bytes 221192 | tf_op jit(solution)/shard_map/ppermute | solution.py:281
  32.0 0.5 %collective-permute-done.10.refs_1_ = f32[144,128]{1,0:T(8,128)S(1)} collective-permute-done((f32[144,128]{1,0:T(8,128)S(1)}, f32[144,128]{1,0:T(8,128)S(1)}, u32[]{:S(2)}, u32[]{:S(2)}) %collective-permute-start.10) | collective-permute-done | bytes 73760 | tf_op jit(solution)/shard_map/ppermute | solution.py:281
  32.4 4.4 %collective-permute-done.11.refs_2_ = f32[144,128]{1,0:T(8,128)S(1)} collective-permute-done((f32[144,128]{1,0:T(8,128)S(1)}, f32[144,128]{1,0:T(8,128)S(1)}, u32[]{:S(2)}, u32[]{:S(2)}) %collective-permute-start.11) | collective-permute-done | bytes 73760 | tf_op jit(solution)/shard_map/ppermute | solution.py:281
  36.9 1.0 %shard_map.48 = f32[2,4,32]{2,1,0:T(4,128)} custom-call(f32[2,128]{1,0:T(2,128)S(1)} %broadcast_in_dim.4.inverse_ref, f32[144,128]{1,0:T(8,128)S(1)} %shard_map.47.refs_0_, f32[144,128]{1,0:T(8,128)S(1)} %collective-permute-done.10.refs_1_, f32[144,128]{1,0:T(8,128)S(1)} %collective-permute-done.11.refs_2_, f32[144,128]{1,0:T(8,128)S(1)} %collective-permute-done.12.refs_3_), custom_call_target="tpu_custom_call" | custom-call | tf_op jit(solution)/shard_map/pallas_call | solution.py:292
  (14 shorter events, 0.2 us)
Async XLA Ops:
  0.0 0.7 %copy-start = (s32[2,4]{1,0:T(2,128)S(1)}, s32[2,4]{1,0:T(2,128)}, u32[]{:S(2)}) copy-start(s32[2,4]{1,0:T(2,128)} %assign_hbm.1) | copy-start | bytes 100
  1.8 16.4 %collective-permute-start.1 = (f32[136,256]{1,0:T(8,128)S(1)}, f32[136,256]{1,0:T(8,128)S(1)}, u32[]{:S(2)}, u32[]{:S(2)}) collective-permute-start(f32[136,256]{1,0:T(8,128)S(1)} %prepare.1.refs_0_.refs_4_), channel_id=1, source_target_pairs={{0,8},{4,12},{8,0},{12,4},{16,24},{20,28},{24,16},{28,20},{1,9},{5... | collective-permute-start | bytes 417800 | tf_op jit(solution)/shard_map/ppermute | solution.py:281
  4.8 13.3 %collective-permute-start = (f32[136,256]{1,0:T(8,128)S(1)}, f32[136,256]{1,0:T(8,128)S(1)}, u32[]{:S(2)}, u32[]{:S(2)}) collective-permute-start(f32[136,256]{1,0:T(8,128)S(1)} %prepare.1.refs_0_.refs_4_), channel_id=1, source_target_pairs={{0,4},{4,0},{8,12},{12,8},{16,20},{20,16},{24,28},{28,24},{1,5},{5... | collective-permute-start | bytes 417800 | tf_op jit(solution)/shard_map/ppermute | solution.py:281
  4.8 9.8 %collective-permute-start.3 = (f32[128,256]{1,0:T(8,128)}, f32[128,256]{1,0:T(8,128)S(1)}, u32[]{:S(2)}, u32[]{:S(2)}) collective-permute-start(f32[128,256]{1,0:T(8,128)} %bitcast.x_hbm), channel_id=1, source_target_pairs={{0,2},{1,3},{2,0},{3,1},{4,6},{5,7},{6,4},{7,5},{8,10},{9,11},{10,... | collective-permute-start | bytes 393224 | tf_op jit(solution)/shard_map/ppermute | solution.py:281
  7.4 10.8 %collective-permute-start.4 = (f32[136,256]{1,0:T(8,128)S(1)}, f32[136,256]{1,0:T(8,128)S(1)}, u32[]{:S(2)}, u32[]{:S(2)}) collective-permute-start(f32[136,256]{1,0:T(8,128)S(1)} %prepare.1.refs_0_.refs_4_), channel_id=1, source_target_pairs={{0,16},{4,20},{8,24},{12,28},{16,0},{20,4},{24,8},{28,12},{1,17},{... | collective-permute-start | bytes 417800 | tf_op jit(solution)/shard_map/ppermute | solution.py:281
  8.9 9.8 %collective-permute-start.6 = (f32[136,256]{1,0:T(8,128)S(1)}, f32[136,256]{1,0:T(8,128)S(1)}, u32[]{:S(2)}, u32[]{:S(2)}) collective-permute-start(f32[136,256]{1,0:T(8,128)S(1)} %prepare.1.refs_0_.refs_4_), channel_id=1, source_target_pairs={{0,24},{4,28},{8,16},{12,20},{16,8},{20,12},{24,0},{28,4},{1,25},{... | collective-permute-start | bytes 417800 | tf_op jit(solution)/shard_map/ppermute | solution.py:281
  14.6 8.4 %collective-permute-start.8 = (f32[128,256]{1,0:T(8,128)}, f32[128,256]{1,0:T(8,128)S(1)}, u32[]{:S(2)}, u32[]{:S(2)}) collective-permute-start(f32[128,256]{1,0:T(8,128)} %bitcast.x_hbm), channel_id=1, source_target_pairs={{0,3},{1,2},{2,1},{3,0},{4,7},{5,6},{6,5},{7,4},{8,11},{9,10},{10,... | collective-permute-start | bytes 393224 | tf_op jit(solution)/shard_map/ppermute | solution.py:281
  18.1 6.9 %collective-permute-start.9 = (f32[128,256]{1,0:T(8,128)}, f32[128,256]{1,0:T(8,128)S(1)}, u32[]{:S(2)}, u32[]{:S(2)}) collective-permute-start(f32[128,256]{1,0:T(8,128)} %bitcast.x_hbm), channel_id=1, source_target_pairs={{0,1},{1,0},{2,3},{3,2},{4,5},{5,4},{6,7},{7,6},{8,9},{9,8},{10,11... | collective-permute-start | bytes 393224 | tf_op jit(solution)/shard_map/ppermute | solution.py:281
  18.1 1.4 %collective-permute-start.2 = (f32[136,256]{1,0:T(8,128)S(1)}, f32[136,256]{1,0:T(8,128)S(1)}, u32[]{:S(2)}, u32[]{:S(2)}) collective-permute-start(f32[136,256]{1,0:T(8,128)S(1)} %collective-permute-done.1.refs_2_), channel_id=1, source_target_pairs={{0,4},{4,0},{8,12},{12,8},{16,20},{20,16},{24,28},{28,24},{1,5},{5... | collective-permute-start | bytes 417800 | tf_op jit(solution)/shard_map/ppermute | solution.py:281
  18.2 6.8 %collective-permute-start.5 = (f32[136,256]{1,0:T(8,128)S(1)}, f32[136,256]{1,0:T(8,128)S(1)}, u32[]{:S(2)}, u32[]{:S(2)}) collective-permute-start(f32[136,256]{1,0:T(8,128)S(1)} %collective-permute-done.4.refs_4_), channel_id=1, source_target_pairs={{0,4},{4,0},{8,12},{12,8},{16,20},{20,16},{24,28},{28,24},{1,5},{5... | collective-permute-start | bytes 417800 | tf_op jit(solution)/shard_map/ppermute | solution.py:281
  18.7 6.3 %collective-permute-start.7 = (f32[136,256]{1,0:T(8,128)S(1)}, f32[136,256]{1,0:T(8,128)S(1)}, u32[]{:S(2)}, u32[]{:S(2)}) collective-permute-start(f32[136,256]{1,0:T(8,128)S(1)} %collective-permute-done.6.refs_6_), channel_id=1, source_target_pairs={{0,4},{4,0},{8,12},{12,8},{16,20},{20,16},{24,28},{28,24},{1,5},{5... | collective-permute-start | bytes 417800 | tf_op jit(solution)/shard_map/ppermute | solution.py:281
  27.5 4.9 %collective-permute-start.10 = (f32[144,128]{1,0:T(8,128)S(1)}, f32[144,128]{1,0:T(8,128)S(1)}, u32[]{:S(2)}, u32[]{:S(2)}) collective-permute-start(f32[144,128]{1,0:T(8,128)S(1)} %shard_map.47.refs_0_), channel_id=1, source_target_pairs={{0,1},{1,0},{2,3},{3,2},{4,5},{5,4},{6,7},{7,6},{8,9},{9,8},{10,11... | collective-permute-start | bytes 221192 | tf_op jit(solution)/shard_map/ppermute | solution.py:281
  29.2 7.7 %collective-permute-start.11 = (f32[144,128]{1,0:T(8,128)S(1)}, f32[144,128]{1,0:T(8,128)S(1)}, u32[]{:S(2)}, u32[]{:S(2)}) collective-permute-start(f32[144,128]{1,0:T(8,128)S(1)} %shard_map.47.refs_0_), channel_id=1, source_target_pairs={{0,2},{1,3},{2,0},{3,1},{4,6},{5,7},{6,4},{7,5},{8,10},{9,11},{10,... | collective-permute-start | bytes 221192 | tf_op jit(solution)/shard_map/ppermute | solution.py:281
  29.8 7.1 %collective-permute-start.12 = (f32[144,128]{1,0:T(8,128)S(1)}, f32[144,128]{1,0:T(8,128)S(1)}, u32[]{:S(2)}, u32[]{:S(2)}) collective-permute-start(f32[144,128]{1,0:T(8,128)S(1)} %shard_map.47.refs_0_), channel_id=1, source_target_pairs={{0,3},{1,2},{2,1},{3,0},{4,7},{5,6},{6,5},{7,4},{8,11},{9,10},{10,... | collective-permute-start | bytes 221192 | tf_op jit(solution)/shard_map/ppermute | solution.py:281
where the time goes:
time: 38 us; the launch traced here: 37.8 us
  starting transfers between devices  16.2 us (43%)
  waiting for transfers between devices  13.8 us (36%)
  Pallas kernels  5.54 us (15%)
  other arithmetic  1.43 us (4%)
  local copies, waits for them, and re-layouts  0.83 us (2%)
    ppermute x13, starting transfers between devices, over(): return lax.ppermute(value, axis, [(i, i ^ k) for i in range(size)])  16.2 us
    ppermute x13, waiting for transfers between devices, over(): return lax.ppermute(value, axis, [(i, i ^ k) for i in range(size)])  13.8 us
    pallas_call x3, Pallas kernels, call(): pl.pallas_call(functools.partial(kernel, **sizes), out_shape=outs[0] if o...  4.45 us
    pallas_call x1, Pallas kernels, program(): pl.pallas_call(functools.partial(prepare_kernel, subs=subs, rows=rows, ro...  1.09 us
  transfers between devices with their start and end apart: 13, of which 6 were waited for; matrix products, arithmetic and copies ran while one was open for 4% of the time, Pallas kernels for 3%

commit v1 on v0

--- a/solution.py
+++ b/solution.py
@@ -33,23 +33,66 @@
             stack[i * size : (i + 1) * size, at : at + value.shape[1]] = parts[k]
 
 
-def prepare_kernel(first_ref, assign_hbm, x_hbm, out_ref, assign_ref, sems, *, subs, rows, rounds):
-    lanes = subs * rows
-    assign = pltpu.make_async_copy(assign_hbm, assign_ref, sems.at[0])
-    assign.start()
-    load = pltpu.make_async_copy(x_hbm, out_ref.at[pl.ds(0, lanes)], sems.at[1])
-    load.start()
+def prepare_kernel(
+    assign_hbm,
+    table_hbm,
+    band_hbm,
+    x_hbm,
+    out_ref,
+    hot_ref,
+    inverse_ref,
+    assign_ref,
+    table_ref,
+    band_ref,
+    sems,
+    *,
+    subs,
+    rows,
+    rounds,
+    pairs,
+):
+    lanes = subs * rows
+    width = out_ref.shape[1]
+    copies = [
+        pltpu.make_async_copy(source, target, sems.at[i])
+        for i, (source, target) in enumerate(
+            (
+                (assign_hbm, assign_ref),
+                (band_hbm, band_ref),
+                (table_hbm, table_ref),
+                (x_hbm, out_ref.at[pl.ds(0, lanes)]),
+            )
+        )
+    ]
+    for copy in copies:
+        copy.start()
+    for copy in copies[:-1]:
+        copy.wait()
+    block, first = lax.axis_index("blk"), lax.axis_index("grp") * rows
     lane = lax.broadcasted_iota(jnp.int32, (8, lanes), 1)
     line = lax.broadcasted_iota(jnp.int32, (8, lanes), 0)
-    own = lane % rows + first_ref[...]
-    assign.wait()
     weight = jnp.zeros((8, lanes), jnp.float32)
     for turn in range(rounds):
         for sub in range(subs):
-            mine = (line == turn) & (lane // rows == sub)
-            chosen = assign_ref[turn : turn + 1, sub : sub + 1]
-            weight = jnp.where(mine & (own == chosen), 1.0, weight)
-    load.wait()
+            local = assign_ref[turn, sub] - first
+            inside = jnp.logical_and(local >= 0, local < rows)
+            target = jnp.where(inside, sub * rows + local, -1)
+            weight = jnp.where((line == turn) & (lane == target), 1.0, weight)
+        index = jnp.full((1, lanes), band_ref[turn], jnp.int32).astype(jnp.float32)
+        band_sq = width * (1.0 + index / 256.0) / 32.0
+        inverse_ref[turn : turn + 1, :] = 1.0 / (2.0 * band_sq)
+    members = hot_ref.shape[1]
+    column = lax.broadcasted_iota(jnp.int32, (8, members), 1)
+    line = lax.broadcasted_iota(jnp.int32, (8, members), 0)
+    for base in range(0, subs * pairs, 8):
+        target = jnp.zeros((8, members), jnp.int32)
+        for i in range(8):
+            entry = table_ref[(base + i) // pairs, (base + i) % pairs]
+            owner = lax.div(entry, jnp.int32(subs))
+            at = (owner ^ block) * subs + (entry - owner * subs)
+            target = jnp.where(line == i, at, target)
+        hot_ref[base : base + 8, :] = (column == target).astype(jnp.float32)
+    copies[-1].wait()
     out_ref[lanes:, :] = lax.dot_general(
         weight, out_ref[:lanes, :], NN, precision=HIGH, preferred_element_type=jnp.float32
     )
@@ -125,19 +168,47 @@
     )
 
 
+def middle_kernel(
+    inverse_ref, stack, low_ref, totals_ref, *refs, near, chunks, subs, rows, rounds
+):
+    lanes = subs * rows
+    key_refs = refs[:near]
+    query_refs = refs[near : near + chunks]
+    terms, norm, low, totals = refs[near + chunks :]
+    before = low_ref.shape[1]
+    count = low.shape[1]
+    low[:, :before] = low_ref[...]
+    totals[:, :, :before] = totals_ref[...]
+    take_queries(query_refs, lanes, terms, norm)
+    scan(
+        inverse_ref,
+        key_refs,
+        stack,
+        terms,
+        low,
+        totals,
+        first=0,
+        columns=slice(before, count),
+        subs=subs,
+        rows=rows,
+        rounds=rounds,
+    )
+
+
 def score_kernel(
     inverse_ref,
     hot_ref,
+    picked_ref,
     near_terms,
     near_norm,
-    near_stack,
+    far_terms,
+    far_norm,
     near_low,
     near_totals,
     *refs,
     chunks,
     later,
     near,
-    blocks,
     groups,
     subs,
     rows,
@@ -145,41 +216,42 @@
     pairs,
     members,
 ):
-    key_refs = refs[:blocks]
-    query_refs = refs[blocks : blocks + len(later)]
-    out_ref, terms, norm, stack, low, totals = refs[blocks + len(later) :]
+    out_ref, stack, low, totals = refs[-4:]
+    key_refs = refs[:-4]
     lanes = subs * rows
     width = key_refs[0].shape[1]
     before = len(chunks) * lanes
     count = before + len(later) * lanes
     cross_at, norm_at, centre_at, _ = layout(groups, rounds, pairs, width, lanes)
-    sizes = {"subs": subs, "rows": rows, "rounds": rounds}
-    old, new = slice(0, before), slice(before, count)
-    take_keys(key_refs[near:], lanes, stack)
-    scan(
-        inverse_ref, key_refs[near:], stack, near_terms, low, totals, first=near, columns=old, **sizes
-    )
-    take_queries(query_refs, lanes, terms, norm)
-    scan(
-        inverse_ref, key_refs[:near], near_stack, terms, low, totals, first=0, columns=new, **sizes
-    )
-    scan(
-        inverse_ref, key_refs[near:], stack, terms, low, totals, first=near, columns=new, **sizes
-    )
+    take_keys(key_refs, lanes, stack)
+    for terms, columns in ((near_terms, slice(0, before)), (far_terms, slice(before, count))):
+        scan(
+            inverse_ref,
+            key_refs,
+            stack,
+            terms,
+            low,
+            totals,
+            first=near,
+            columns=columns,
+            subs=subs,
+            rows=rows,
+            rounds=rounds,
+        )
     done = near * subs
-    low[:done, old] = near_low[...]
-    totals[:, :done, old] = near_totals[...]
-    centre = sum(ref[lanes:, :] for ref in key_refs) / members
+    low[:done, :] = near_low[...]
+    totals[:, :done, :] = near_totals[...]
+    centre = picked_ref[...] / members
     a = split(centre)
     left = jnp.concatenate([a[k] for k in LEFT], 1)
     cross = jnp.concatenate(
         [
             lax.dot_general(left, right[...], NN, preferred_element_type=jnp.float32)
-            for right in (near_terms, terms)
+            for right in (near_terms, far_terms)
         ],
         1,
     )
-    query_norm = jnp.concatenate([near_norm[:1, :], norm[:1, :]], 1)
+    query_norm = jnp.concatenate([near_norm[:1, :], far_norm[:1, :]], 1)
     nearest = low[...] + query_norm
     hot = hot_ref[...]
     lane = lax.broadcasted_iota(jnp.int32, (pairs, lanes), 1) // rows
@@ -274,14 +346,12 @@
     blocks = lax.axis_size("blk")
     members = subs * blocks
     lanes = subs * rows
-    group = lax.axis_index("grp")
-    block = lax.axis_index("blk")
 
     def over(axis, size, value, k):
         return lax.ppermute(value, axis, [(i, i ^ k) for i in range(size)])
 
     vmem = pl.BlockSpec(memory_space=pltpu.VMEM)
-    hbm = pl.BlockSpec(memory_space=pl.ANY)
+    hbm = pl.BlockSpec(memory_space=pltpu.HBM)
 
     def call(kernel, shapes, arrays, scratch=(), **sizes):
         one = not isinstance(shapes, list)
@@ -303,37 +373,48 @@
     f32, bf16 = jnp.float32, jnp.bfloat16
     x = samples.reshape(lanes, width)
     queries = {k: over("grp", groups, x, k) for k in range(groups - 1, 0, -1)}
-    own = pl.pallas_call(
-        functools.partial(prepare_kernel, subs=subs, rows=rows, rounds=rounds),
-        out_shape=jax.ShapeDtypeStruct((lanes + 8, width), f32),
-        in_specs=[vmem, hbm, hbm],
-        out_specs=vmem,
+    own, hot, inverse = pl.pallas_call(
+        functools.partial(prepare_kernel, subs=subs, rows=rows, rounds=rounds, pairs=pairs),
+        out_shape=[
+            jax.ShapeDtypeStruct((lanes + 8, width), f32),
+            jax.ShapeDtypeStruct((subs * pairs, members), f32),
+            jax.ShapeDtypeStruct((rounds, lanes), f32),
+        ],
+        in_specs=[hbm] * 4,
+        out_specs=[vmem] * 3,
         scratch_shapes=[
-            pltpu.VMEM((rounds, subs), jnp.int32),
-            pltpu.SemaphoreType.DMA((2,)),
+            pltpu.SMEM((rounds, subs), jnp.int32),
+            pltpu.SMEM((subs, pairs), jnp.int32),
+            pltpu.SMEM((rounds,), jnp.int32),
+            pltpu.SemaphoreType.DMA((4,)),
         ],
         compiler_params=pltpu.CompilerParams(vmem_limit_bytes=4 * 2**20),
         name="prepare",
-    )(jnp.full((1, lanes), group * rows, jnp.int32), assignment, x)
+    )(
+        *[
+            pltpu.with_memory_space_constraint(value, pltpu.HBM)
+            for value in (assignment, pair_table, band_index, x)
+        ]
+    )
     keys = {0: own}
     for k in range(2, blocks, 2):
-        keys[k] = over("blk", blocks, own, k)
+        keys[k] = over("blk", blocks, own if k > 2 else x, k)
     for k in range(0, blocks, 2):
-        keys[k ^ 1] = over("blk", blocks, keys[k], 1)
+        sent = keys[k] if k else x
+        keys[k ^ 1] = over("blk", blocks, sent, 1)
+    picked = own[lanes:]
+    others = [over("blk", blocks, picked, k) for k in range(2, 4, 2)]
+    picked = sum(others, picked)
+    picked = picked + over("blk", blocks, picked, 1)
+    picked = sum([keys[k][lanes:] for k in range(4, blocks)], picked)
     queries[0] = own
-    place = (pair_table // subs ^ block) * subs + pair_table % subs
-    hot = (
-        place.reshape(subs * pairs, 1) == jnp.arange(members, dtype=jnp.int32)[None, :]
-    ).astype(f32)
-    band_sq = width * (1.0 + band_index.astype(f32) / 256.0) / 32.0
-    inverse = jnp.broadcast_to((1.0 / (2.0 * band_sq))[:, None], (rounds, lanes))
     height = layout(groups, rounds, pairs, width, lanes)[-1]
     order = CHUNKS if groups == len(CHUNKS) else tuple(range(groups))
     chunks, later = order[: groups // 2], order[groups // 2 :]
     near = blocks // 2
     before, after = len(chunks) * lanes, len(later) * lanes
     sizes = {"subs": subs, "rows": rows, "rounds": rounds}
-    known = call(
+    near_terms, near_norm, stack, low, totals = call(
         early_kernel,
         [
             (len(RIGHT) * width, before, bf16),
@@ -347,15 +428,27 @@
         chunks=len(chunks),
         **sizes,
     )
+    far_terms, far_norm, low, totals = call(
+        middle_kernel,
+        [
+            (len(RIGHT) * width, after, bf16),
+            (8, after, f32),
+            (near * subs, before + after, f32),
+            (rounds, near * subs, before + after, f32),
+        ],
+        [inverse, stack, low, totals]
+        + [keys[k] for k in range(near)]
+        + [queries[k] for k in later],
+        near=near,
+        chunks=len(later),
+        **sizes,
+    )
     part = call(
         score_kernel,
         (height, lanes, f32),
-        [inverse, hot, *known]
-        + [keys[k] for k in range(blocks)]
-        + [queries[k] for k in later],
+        [inverse, hot, picked, near_terms, near_norm, far_terms, far_norm, low, totals]
+        + [keys[k] for k in range(near, blocks)],
         scratch=[
-            (len(RIGHT) * width, after, bf16),
-            (8, after, f32),
             ((blocks - near) * lanes, len(LEFT) * width, bf16),
             (members, before + after, f32),
             (rounds, members, before + after, f32),
@@ -363,7 +456,6 @@
         chunks=chunks,
         later=later,
         near=near,
-        blocks=blocks,
         groups=groups,
         pairs=pairs,
         members=members,

time: 38 us -> 37.3 us (0.982)
  starting transfers between devices: 16.2 us -> 17.9 us
  other arithmetic: 1.43 us -> 0.01 us
  local copies, waits for them, and re-layouts: 0.83 us -> 0.01 us
  waiting for transfers between devices: 13.8 us -> 13.4 us
    ppermute x13 -> x15, starting transfers between devices: 16.2 us -> 17.9 us  [over(): return lax.ppermute(value, axis, [(i, i ^ k) for i in range(size)])]
    add x1 -> x2, other arithmetic: 0.69 us -> 0.01 us  [the longest x1 0.01 us: program(): picked = sum([keys[k][lanes:] for k in range(4, blocks)], picked)]
    unnamed x2 -> x0, local copies, waits for them, and re-layouts: 0.68 us -> none
    div x1 -> x0, other arithmetic: 0.66 us -> none  [program(): 1.0 / (2.0 * band_sq)]
    ppermute x13 -> x15, waiting for transfers between devices: 13.8 us -> 13.4 us  [over(): return lax.ppermute(value, axis, [(i, i ^ k) for i in range(size)])]
    pallas_call x3 -> x4, Pallas kernels: 4.45 us -> 4.62 us  [call(): pl.pallas_call(functools.partial(kernel, **sizes), out_shape=outs[0] if o...]
  transfers between devices with their start and end apart: 13 -> 15, of which waited for: 6 -> 6; matrix products, arithmetic and copies ran while one was open for 4% -> 0% of each run, Pallas kernels for 3% -> 5%
where the time goes in v1:
time: 37.3 us; the launch traced here: 37.1 us
  starting transfers between devices  17.9 us (48%)
  waiting for transfers between devices  13.4 us (36%)
  Pallas kernels  5.76 us (15%)
    ppermute x15, starting transfers between devices, over(): return lax.ppermute(value, axis, [(i, i ^ k) for i in range(size)])  17.9 us
    ppermute x15, waiting for transfers between devices, over(): return lax.ppermute(value, axis, [(i, i ^ k) for i in range(size)])  13.4 us
    pallas_call x4, Pallas kernels, call(): pl.pallas_call(functools.partial(kernel, **sizes), out_shape=outs[0] if o...  4.62 us
    pallas_call x1, Pallas kernels, program(): pl.pallas_call(functools.partial(prepare_kernel, subs=subs, rows=rows, ro...  1.14 us
  transfers between devices with their start and end apart: 15, of which 6 were waited for; matrix products, arithmetic and copies ran while one was open for 0% of the time, Pallas kernels for 5%

profile of v1, /device:TPU:0, one launch (start us, length us, event | category | flops | bytes accessed | tf_op | source)
XLA Modules:
  0.0 37.1 jit_solution(14316268004492145967)
XLA Ops:
  0.0 1.1 %prepare.1 = (f32[136,256]{1,0:T(8,128)S(1)}, f32[64,32]{1,0:T(8,128)S(1)}, f32[2,128]{1,0:T(2,128)S(1)}) custom-call(s32[2,4]{1,0:T(2,128)} %assign_hbm.1, s32[4,16]{1,0:T(4,128)} %table_hbm.1, s32[2]{0:T(128)} %band_hbm.1, f32[128,256]{1,0:T(8,128)} %bitcast.1), custom_call_target="tpu_custom_call" | custom-call | tf_op jit(solution)/shard_map/prepare/pallas_call | solution.py:376
  1.2 3.0 %collective-permute-start = (f32[8,256]{1,0:T(8,128)S(1)}, f32[8,256]{1,0:T(8,128)S(1)}, u32[]{:S(2)}, u32[]{:S(2)}) collective-permute-start(f32[8,256]{1,0:T(8,128)S(1)} %slice.15), channel_id=1, source_target_pairs={{0,8},{4,12},{8,0},{12,4},{16,24},{20,28},{24,16},{28,20},{1,9},{5... | collective-permute-start | bytes 24584 | tf_op jit(solution)/shard_map/ppermute | solution.py:351
  4.2 1.5 %collective-permute-start.2 = (f32[136,256]{1,0:T(8,128)S(1)}, f32[136,256]{1,0:T(8,128)S(1)}, u32[]{:S(2)}, u32[]{:S(2)}) collective-permute-start(f32[136,256]{1,0:T(8,128)S(1)} %get-tuple-element.19.refs_0_.refs_4_), channel_id=1, source_target_pairs={{0,16},{4,20},{8,24},{12,28},{16,0},{20,4},{24,8},{28,12},{1,17},{... | collective-permute-start | bytes 417800 | tf_op jit(solution)/shard_map/ppermute | solution.py:351
  5.7 0.0 collective-permute-start.4
  5.7 1.9 %collective-permute-start.7 = (f32[128,256]{1,0:T(8,128)}, f32[128,256]{1,0:T(8,128)S(1)}, u32[]{:S(2)}, u32[]{:S(2)}) collective-permute-start(f32[128,256]{1,0:T(8,128)} %bitcast.2), channel_id=1, source_target_pairs={{0,8},{4,12},{8,0},{12,4},{16,24},{20,28},{24,16},{28,20},{1,9},{5... | collective-permute-start | bytes 393224 | tf_op jit(solution)/shard_map/ppermute | solution.py:351
  7.7 0.0 collective-permute-start.6
  7.7 2.6 %collective-permute-start.9 = (f32[128,256]{1,0:T(8,128)}, f32[128,256]{1,0:T(8,128)S(1)}, u32[]{:S(2)}, u32[]{:S(2)}) collective-permute-start(f32[128,256]{1,0:T(8,128)} %bitcast.4), channel_id=1, source_target_pairs={{0,2},{1,3},{2,0},{3,1},{4,6},{5,7},{6,4},{7,5},{8,10},{9,11},{10,... | collective-permute-start | bytes 393224 | tf_op jit(solution)/shard_map/ppermute | solution.py:351
  10.3 3.1 %collective-permute-done.7.refs_2_ = f32[128,256]{1,0:T(8,128)S(1)} collective-permute-done((f32[128,256]{1,0:T(8,128)}, f32[128,256]{1,0:T(8,128)S(1)}, u32[]{:S(2)}, u32[]{:S(2)}) %collective-permute-start.7) | collective-permute-done | bytes 131104 | tf_op jit(solution)/shard_map/ppermute | solution.py:351
  13.4 3.6 %collective-permute-start.10 = (f32[128,256]{1,0:T(8,128)}, f32[128,256]{1,0:T(8,128)S(1)}, u32[]{:S(2)}, u32[]{:S(2)}) collective-permute-start(f32[128,256]{1,0:T(8,128)} %bitcast.5), channel_id=1, source_target_pairs={{0,3},{1,2},{2,1},{3,0},{4,7},{5,6},{6,5},{7,4},{8,11},{9,10},{10,... | collective-permute-start | bytes 393224 | tf_op jit(solution)/shard_map/ppermute | solution.py:351
  17.0 2.8 %collective-permute-done.9.refs_5_ = f32[128,256]{1,0:T(8,128)S(1)} collective-permute-done((f32[128,256]{1,0:T(8,128)}, f32[128,256]{1,0:T(8,128)S(1)}, u32[]{:S(2)}, u32[]{:S(2)}) %collective-permute-start.9) | collective-permute-done | bytes 131104 | tf_op jit(solution)/shard_map/ppermute | solution.py:351
  19.8 0.5 %collective-permute-start.3 = (f32[136,256]{1,0:T(8,128)S(1)}, f32[136,256]{1,0:T(8,128)S(1)}, u32[]{:S(2)}, u32[]{:S(2)}) collective-permute-start(f32[136,256]{1,0:T(8,128)S(1)} %collective-permute-done.2.refs_0_), channel_id=1, source_target_pairs={{0,4},{4,0},{8,12},{12,8},{16,20},{20,16},{24,28},{28,24},{1,5},{5... | collective-permute-start | bytes 417800 | tf_op jit(solution)/shard_map/ppermute | solution.py:351
  20.3 0.1 collective-permute-start.5
  20.4 0.8 %collective-permute-done.8.refs_3_ = f32[128,256]{1,0:T(8,128)S(1)} collective-permute-done((f32[128,256]{1,0:T(8,128)S(1)}, f32[128,256]{1,0:T(8,128)S(1)}, u32[]{:S(2)}, u32[]{:S(2)}) %collective-permute-start.8) | collective-permute-done | bytes 131104 | tf_op jit(solution)/shard_map/ppermute | solution.py:351
  21.2 0.1 collective-permute-start.1
  21.3 1.0 %shard_map.46 = (bf16[1536,256]{1,0:T(8,128)(2,1)S(1)}, f32[8,256]{1,0:T(8,128)S(1)}, bf16[512,1536]{1,0:T(8,128)(2,1)S(1)}, f32[16,256]{1,0:T(8,128)S(1)}, f32[2,16,256]{2,1,0:T(8,128)S(1)}) custom-call(f32[2,128]{1,0:T(2,128)S(1)} %get-tuple-element.17.inverse_ref, f32[136,256]{1,0:T(8,128)S(1)} %get-tuple-element.19.refs_0_.refs_4_, ...), custom_call_target="tpu_custom_call" | custom-call | tf_op jit(solution)/shard_map/pallas_call | solution.py:362
  22.3 0.8 %collective-permute-done.11.refs_5_ = f32[128,256]{1,0:T(8,128)S(1)} collective-permute-done((f32[128,256]{1,0:T(8,128)}, f32[128,256]{1,0:T(8,128)S(1)}, u32[]{:S(2)}, u32[]{:S(2)}) %collective-permute-start.11) | collective-permute-done | bytes 131104 | tf_op jit(solution)/shard_map/ppermute | solution.py:351
  23.1 0.9 %shard_map.47 = (bf16[1536,256]{1,0:T(8,128)(2,1)S(1)}, f32[8,256]{1,0:T(8,128)S(1)}, f32[16,512]{1,0:T(8,128)S(1)}, f32[2,16,512]{2,1,0:T(8,128)S(1)}) custom-call(f32[2,128]{1,0:T(2,128)S(1)} %get-tuple-element.17.inverse_ref, bf16[512,1536]{1,0:T(8,128)(2,1)S(1)} %get-tuple-element.22.stack, f32[16,256]{1,0:T(8,128)S(1)} %get-tuple-element.23.low_ref, ...), custom_call_target="tpu_custom_call" | custom-call | tf_op jit(solution)/shard_map/pallas_call | solution.py:362
  24.1 1.8 %shard_map.48.refs_0_ = f32[144,128]{1,0:T(8,128)S(1)} custom-call(f32[2,128]{1,0:T(2,128)S(1)} %get-tuple-element.17.inverse_ref, f32[64,32]{1,0:T(8,128)S(1)} %get-tuple-element.18.hot_ref, f32[8,256]{1,0:T(8,128)S(1)} %slice_add_fusion.picked_ref, bf16[1536,256]{1,0:T(8,128)(2,1)S(1)} %get-tuple-element.20.near_terms, ...), custom_call_target="tpu_custom_call" | custom-call | tf_op jit(solution)/shard_map/pallas_call | solution.py:362
  25.9 0.9 %collective-permute-start.12 = (f32[144,128]{1,0:T(8,128)S(1)}, f32[144,128]{1,0:T(8,128)S(1)}, u32[]{:S(2)}, u32[]{:S(2)}) collective-permute-start(f32[144,128]{1,0:T(8,128)S(1)} %shard_map.48.refs_0_), channel_id=1, source_target_pairs={{0,1},{1,0},{2,3},{3,2},{4,5},{5,4},{6,7},{7,6},{8,9},{9,8},{10,11... | collective-permute-start | bytes 221192 | tf_op jit(solution)/shard_map/ppermute | solution.py:351
  26.8 3.2 %collective-permute-start.13 = (f32[144,128]{1,0:T(8,128)S(1)}, f32[144,128]{1,0:T(8,128)S(1)}, u32[]{:S(2)}, u32[]{:S(2)}) collective-permute-start(f32[144,128]{1,0:T(8,128)S(1)} %shard_map.48.refs_0_), channel_id=1, source_target_pairs={{0,2},{1,3},{2,0},{3,1},{4,6},{5,7},{6,4},{7,5},{8,10},{9,11},{10,... | collective-permute-start | bytes 221192 | tf_op jit(solution)/shard_map/ppermute | solution.py:351
  29.9 0.4 %collective-permute-start.14 = (f32[144,128]{1,0:T(8,128)S(1)}, f32[144,128]{1,0:T(8,128)S(1)}, u32[]{:S(2)}, u32[]{:S(2)}) collective-permute-start(f32[144,128]{1,0:T(8,128)S(1)} %shard_map.48.refs_0_), channel_id=1, source_target_pairs={{0,3},{1,2},{2,1},{3,0},{4,7},{5,6},{6,5},{7,4},{8,11},{9,10},{10,... | collective-permute-start | bytes 221192 | tf_op jit(solution)/shard_map/ppermute | solution.py:351
  30.3 4.8 %collective-permute-done.13.refs_2_ = f32[144,128]{1,0:T(8,128)S(1)} collective-permute-done((f32[144,128]{1,0:T(8,128)S(1)}, f32[144,128]{1,0:T(8,128)S(1)}, u32[]{:S(2)}, u32[]{:S(2)}) %collective-permute-start.13) | collective-permute-done | bytes 73760 | tf_op jit(solution)/shard_map/ppermute | solution.py:351
  35.1 1.0 %collective-permute-done.14.refs_3_ = f32[144,128]{1,0:T(8,128)S(1)} collective-permute-done((f32[144,128]{1,0:T(8,128)S(1)}, f32[144,128]{1,0:T(8,128)S(1)}, u32[]{:S(2)}, u32[]{:S(2)}) %collective-permute-start.14) | collective-permute-done | bytes 73760 | tf_op jit(solution)/shard_map/ppermute | solution.py:351
  36.2 1.0 %shard_map.49 = f32[2,4,32]{2,1,0:T(4,128)} custom-call(f32[2,128]{1,0:T(2,128)S(1)} %get-tuple-element.17.inverse_ref, f32[144,128]{1,0:T(8,128)S(1)} %shard_map.48.refs_0_, f32[144,128]{1,0:T(8,128)S(1)} %collective-permute-done.12.refs_1_, f32[144,128]{1,0:T(8,128)S(1)} %collective-permute-done.13.refs_2_, f32[144,128]{1,0:T(8,128)S(1)} %collective-permute-done.14.refs_3_), custom_call_target="tpu_custom_call" | custom-call | tf_op jit(solution)/shard_map/pallas_call | solution.py:362
  (14 shorter events, 0.0 us)
Async XLA Ops:
  1.2 6.5 %collective-permute-start = (f32[8,256]{1,0:T(8,128)S(1)}, f32[8,256]{1,0:T(8,128)S(1)}, u32[]{:S(2)}, u32[]{:S(2)}) collective-permute-start(f32[8,256]{1,0:T(8,128)S(1)} %slice.15), channel_id=1, source_target_pairs={{0,8},{4,12},{8,0},{12,4},{16,24},{20,28},{24,16},{28,20},{1,9},{5... | collective-permute-start | bytes 24584 | tf_op jit(solution)/shard_map/ppermute | solution.py:351
  4.2 15.6 %collective-permute-start.2 = (f32[136,256]{1,0:T(8,128)S(1)}, f32[136,256]{1,0:T(8,128)S(1)}, u32[]{:S(2)}, u32[]{:S(2)}) collective-permute-start(f32[136,256]{1,0:T(8,128)S(1)} %get-tuple-element.19.refs_0_.refs_4_), channel_id=1, source_target_pairs={{0,16},{4,20},{8,24},{12,28},{16,0},{20,4},{24,8},{28,12},{1,17},{... | collective-permute-start | bytes 417800 | tf_op jit(solution)/shard_map/ppermute | solution.py:351
  5.7 14.6 %collective-permute-start.4 = (f32[136,256]{1,0:T(8,128)S(1)}, f32[136,256]{1,0:T(8,128)S(1)}, u32[]{:S(2)}, u32[]{:S(2)}) collective-permute-start(f32[136,256]{1,0:T(8,128)S(1)} %get-tuple-element.19.refs_0_.refs_4_), channel_id=1, source_target_pairs={{0,24},{4,28},{8,16},{12,20},{16,8},{20,12},{24,0},{28,4},{1,25},{... | collective-permute-start | bytes 417800 | tf_op jit(solution)/shard_map/ppermute | solution.py:351
  5.7 7.6 %collective-permute-start.7 = (f32[128,256]{1,0:T(8,128)}, f32[128,256]{1,0:T(8,128)S(1)}, u32[]{:S(2)}, u32[]{:S(2)}) collective-permute-start(f32[128,256]{1,0:T(8,128)} %bitcast.2), channel_id=1, source_target_pairs={{0,8},{4,12},{8,0},{12,4},{16,24},{20,28},{24,16},{28,20},{1,9},{5... | collective-permute-start | bytes 393224 | tf_op jit(solution)/shard_map/ppermute | solution.py:351
  7.7 9.3 %collective-permute-start.6 = (f32[128,256]{1,0:T(8,128)}, f32[128,256]{1,0:T(8,128)S(1)}, u32[]{:S(2)}, u32[]{:S(2)}) collective-permute-start(f32[128,256]{1,0:T(8,128)} %bitcast.3), channel_id=1, source_target_pairs={{0,4},{4,0},{8,12},{12,8},{16,20},{20,16},{24,28},{28,24},{1,5},{5... | collective-permute-start | bytes 393224 | tf_op jit(solution)/shard_map/ppermute | solution.py:351
  7.7 12.1 %collective-permute-start.9 = (f32[128,256]{1,0:T(8,128)}, f32[128,256]{1,0:T(8,128)S(1)}, u32[]{:S(2)}, u32[]{:S(2)}) collective-permute-start(f32[128,256]{1,0:T(8,128)} %bitcast.4), channel_id=1, source_target_pairs={{0,2},{1,3},{2,0},{3,1},{4,6},{5,7},{6,4},{7,5},{8,10},{9,11},{10,... | collective-permute-start | bytes 393224 | tf_op jit(solution)/shard_map/ppermute | solution.py:351
  13.4 8.9 %collective-permute-start.10 = (f32[128,256]{1,0:T(8,128)}, f32[128,256]{1,0:T(8,128)S(1)}, u32[]{:S(2)}, u32[]{:S(2)}) collective-permute-start(f32[128,256]{1,0:T(8,128)} %bitcast.5), channel_id=1, source_target_pairs={{0,3},{1,2},{2,1},{3,0},{4,7},{5,6},{6,5},{7,4},{8,11},{9,10},{10,... | collective-permute-start | bytes 393224 | tf_op jit(solution)/shard_map/ppermute | solution.py:351
  17.0 6.2 %collective-permute-start.11 = (f32[128,256]{1,0:T(8,128)}, f32[128,256]{1,0:T(8,128)S(1)}, u32[]{:S(2)}, u32[]{:S(2)}) collective-permute-start(f32[128,256]{1,0:T(8,128)} %bitcast.6), channel_id=1, source_target_pairs={{0,1},{1,0},{2,3},{3,2},{4,5},{5,4},{6,7},{7,6},{8,9},{9,8},{10,11... | collective-permute-start | bytes 393224 | tf_op jit(solution)/shard_map/ppermute | solution.py:351
  19.8 1.3 %collective-permute-start.8 = (f32[128,256]{1,0:T(8,128)S(1)}, f32[128,256]{1,0:T(8,128)S(1)}, u32[]{:S(2)}, u32[]{:S(2)}) collective-permute-start(f32[128,256]{1,0:T(8,128)S(1)} %collective-permute-done.7.refs_2_), channel_id=1, source_target_pairs={{0,4},{4,0},{8,12},{12,8},{16,20},{20,16},{24,28},{28,24},{1,5},{5... | collective-permute-start | bytes 393224 | tf_op jit(solution)/shard_map/ppermute | solution.py:351
  19.8 4.2 %collective-permute-start.3 = (f32[136,256]{1,0:T(8,128)S(1)}, f32[136,256]{1,0:T(8,128)S(1)}, u32[]{:S(2)}, u32[]{:S(2)}) collective-permute-start(f32[136,256]{1,0:T(8,128)S(1)} %collective-permute-done.2.refs_0_), channel_id=1, source_target_pairs={{0,4},{4,0},{8,12},{12,8},{16,20},{20,16},{24,28},{28,24},{1,5},{5... | collective-permute-start | bytes 417800 | tf_op jit(solution)/shard_map/ppermute | solution.py:351
  20.3 3.7 %collective-permute-start.5 = (f32[136,256]{1,0:T(8,128)S(1)}, f32[136,256]{1,0:T(8,128)S(1)}, u32[]{:S(2)}, u32[]{:S(2)}) collective-permute-start(f32[136,256]{1,0:T(8,128)S(1)} %collective-permute-done.4.refs_2_), channel_id=1, source_target_pairs={{0,4},{4,0},{8,12},{12,8},{16,20},{20,16},{24,28},{28,24},{1,5},{5... | collective-permute-start | bytes 417800 | tf_op jit(solution)/shard_map/ppermute | solution.py:351
  21.2 2.9 %collective-permute-start.1 = (f32[8,256]{1,0:T(8,128)S(1)}, f32[8,256]{1,0:T(8,128)S(1)}, u32[]{:S(2)}, u32[]{:S(2)}) collective-permute-start(f32[8,256]{1,0:T(8,128)S(1)} %slice_add_fusion.4), channel_id=1, source_target_pairs={{0,4},{4,0},{8,12},{12,8},{16,20},{20,16},{24,28},{28,24},{1,5},{5... | collective-permute-start | bytes 24584 | tf_op jit(solution)/shard_map/ppermute | solution.py:351
  25.9 4.5 %collective-permute-start.12 = (f32[144,128]{1,0:T(8,128)S(1)}, f32[144,128]{1,0:T(8,128)S(1)}, u32[]{:S(2)}, u32[]{:S(2)}) collective-permute-start(f32[144,128]{1,0:T(8,128)S(1)} %shard_map.48.refs_0_), channel_id=1, source_target_pairs={{0,1},{1,0},{2,3},{3,2},{4,5},{5,4},{6,7},{7,6},{8,9},{9,8},{10,11... | collective-permute-start | bytes 221192 | tf_op jit(solution)/shard_map/ppermute | solution.py:351
  26.8 8.4 %collective-permute-start.13 = (f32[144,128]{1,0:T(8,128)S(1)}, f32[144,128]{1,0:T(8,128)S(1)}, u32[]{:S(2)}, u32[]{:S(2)}) collective-permute-start(f32[144,128]{1,0:T(8,128)S(1)} %shard_map.48.refs_0_), channel_id=1, source_target_pairs={{0,2},{1,3},{2,0},{3,1},{4,6},{5,7},{6,4},{7,5},{8,10},{9,11},{10,... | collective-permute-start | bytes 221192 | tf_op jit(solution)/shard_map/ppermute | solution.py:351
  29.9 6.3 %collective-permute-start.14 = (f32[144,128]{1,0:T(8,128)S(1)}, f32[144,128]{1,0:T(8,128)S(1)}, u32[]{:S(2)}, u32[]{:S(2)}) collective-permute-start(f32[144,128]{1,0:T(8,128)S(1)} %shard_map.48.refs_0_), channel_id=1, source_target_pairs={{0,3},{1,2},{2,1},{3,0},{4,7},{5,6},{6,5},{7,4},{8,11},{9,10},{10,... | collective-permute-start | bytes 221192 | tf_op jit(solution)/shard_map/ppermute | solution.py:351

commit v2 on v1

--- a/solution.py
+++ b/solution.py
@@ -398,15 +398,10 @@
     )
     keys = {0: own}
     for k in range(2, blocks, 2):
-        keys[k] = over("blk", blocks, own if k > 2 else x, k)
+        keys[k] = over("blk", blocks, own, k)
     for k in range(0, blocks, 2):
-        sent = keys[k] if k else x
-        keys[k ^ 1] = over("blk", blocks, sent, 1)
-    picked = own[lanes:]
-    others = [over("blk", blocks, picked, k) for k in range(2, 4, 2)]
-    picked = sum(others, picked)
-    picked = picked + over("blk", blocks, picked, 1)
-    picked = sum([keys[k][lanes:] for k in range(4, blocks)], picked)
+        keys[k ^ 1] = over("blk", blocks, keys[k], 1)
+    picked = sum([keys[k][lanes:] for k in range(1, blocks)], own[lanes:])
     queries[0] = own
     height = layout(groups, rounds, pairs, width, lanes)[-1]
     order = CHUNKS if groups == len(CHUNKS) else tuple(range(groups))
@@ -474,7 +469,7 @@
     )
 
 
-CHUNKS = (0, 2, 3, 1)
+CHUNKS = (0, 3, 2, 1)
 
 
 def solution(mesh):

time: 37.3 us -> 43.2 us (1.16)
  waiting for transfers between devices: 13.4 us -> 19.9 us
  starting transfers between devices: 17.9 us -> 17.2 us
    ppermute x15 -> x13, waiting for transfers between devices: 13.4 us -> 19.9 us  [over(): return lax.ppermute(value, axis, [(i, i ^ k) for i in range(size)])]
    ppermute x15 -> x13, starting transfers between devices: 17.9 us -> 17.2 us  [over(): return lax.ppermute(value, axis, [(i, i ^ k) for i in range(size)])]
  transfers between devices with their start and end apart: 15 -> 13, of which waited for: 6 -> 8; matrix products, arithmetic and copies ran while one was open for 0% -> 0% of each run, Pallas kernels for 5% -> 2%
where the time goes in v2:
time: 43.2 us; the launch traced here: 43 us
  waiting for transfers between devices  19.9 us (46%)
  starting transfers between devices  17.2 us (40%)
  Pallas kernels  5.78 us (13%)
    ppermute x13, waiting for transfers between devices, over(): return lax.ppermute(value, axis, [(i, i ^ k) for i in range(size)])  19.9 us
    ppermute x13, starting transfers between devices, over(): return lax.ppermute(value, axis, [(i, i ^ k) for i in range(size)])  17.2 us
    pallas_call x4, Pallas kernels, call(): pl.pallas_call(functools.partial(kernel, **sizes), out_shape=outs[0] if o...  4.63 us
    pallas_call x1, Pallas kernels, program(): pl.pallas_call(functools.partial(prepare_kernel, subs=subs, rows=rows, ro...  1.14 us
  transfers between devices with their start and end apart: 13, of which 8 were waited for; matrix products, arithmetic and copies ran while one was open for 0% of the time, Pallas kernels for 2%

profile of v2, /device:TPU:0, one launch (start us, length us, event | category | flops | bytes accessed | tf_op | source)
XLA Modules:
  0.0 43.0 jit_solution(7630556400691334828)
XLA Ops:
  0.0 1.1 %prepare.1 = (f32[136,256]{1,0:T(8,128)S(1)}, f32[64,32]{1,0:T(8,128)S(1)}, f32[2,128]{1,0:T(2,128)S(1)}) custom-call(s32[2,4]{1,0:T(2,128)} %assign_hbm.1, s32[4,16]{1,0:T(4,128)} %table_hbm.1, s32[2]{0:T(128)} %band_hbm.1, f32[128,256]{1,0:T(8,128)} %bitcast.1), custom_call_target="tpu_custom_call" | custom-call | tf_op jit(solution)/shard_map/prepare/pallas_call | solution.py:376
  1.2 3.0 %collective-permute-start.1 = (f32[136,256]{1,0:T(8,128)S(1)}, f32[136,256]{1,0:T(8,128)S(1)}, u32[]{:S(2)}, u32[]{:S(2)}) collective-permute-start(f32[136,256]{1,0:T(8,128)S(1)} %get-tuple-element.19.refs_0_.refs_4_), channel_id=1, source_target_pairs={{0,8},{4,12},{8,0},{12,4},{16,24},{20,28},{24,16},{28,20},{1,9},{5... | collective-permute-start | bytes 417800 | tf_op jit(solution)/shard_map/ppermute | solution.py:351
  4.2 1.5 %collective-permute-start.3 = (f32[136,256]{1,0:T(8,128)S(1)}, f32[136,256]{1,0:T(8,128)S(1)}, u32[]{:S(2)}, u32[]{:S(2)}) collective-permute-start(f32[136,256]{1,0:T(8,128)S(1)} %get-tuple-element.19.refs_0_.refs_4_), channel_id=1, source_target_pairs={{0,16},{4,20},{8,24},{12,28},{16,0},{20,4},{24,8},{28,12},{1,17},{... | collective-permute-start | bytes 417800 | tf_op jit(solution)/shard_map/ppermute | solution.py:351
  5.7 0.0 collective-permute-start.5
  5.7 0.0 collective-permute-start
  5.7 2.5 %collective-permute-done.1.refs_2_ = f32[136,256]{1,0:T(8,128)S(1)} collective-permute-done((f32[136,256]{1,0:T(8,128)S(1)}, f32[136,256]{1,0:T(8,128)S(1)}, u32[]{:S(2)}, u32[]{:S(2)}) %collective-permute-start.1) | collective-permute-done | bytes 139296 | tf_op jit(solution)/shard_map/ppermute | solution.py:351
  8.2 4.1 %collective-permute-done.3.refs_0_ = f32[136,256]{1,0:T(8,128)S(1)} collective-permute-done((f32[136,256]{1,0:T(8,128)S(1)}, f32[136,256]{1,0:T(8,128)S(1)}, u32[]{:S(2)}, u32[]{:S(2)}) %collective-permute-start.3) | collective-permute-done | bytes 139296 | tf_op jit(solution)/shard_map/ppermute | solution.py:351
  12.3 0.5 %collective-permute-start.6 = (f32[136,256]{1,0:T(8,128)S(1)}, f32[136,256]{1,0:T(8,128)S(1)}, u32[]{:S(2)}, u32[]{:S(2)}) collective-permute-start(f32[136,256]{1,0:T(8,128)S(1)} %collective-permute-done.5.refs_2_), channel_id=1, source_target_pairs={{0,4},{4,0},{8,12},{12,8},{16,20},{20,16},{24,28},{28,24},{1,5},{5... | collective-permute-start | bytes 417800 | tf_op jit(solution)/shard_map/ppermute | solution.py:351
  12.8 3.6 %collective-permute-start.7 = (f32[128,256]{1,0:T(8,128)}, f32[128,256]{1,0:T(8,128)S(1)}, u32[]{:S(2)}, u32[]{:S(2)}) collective-permute-start(f32[128,256]{1,0:T(8,128)} %bitcast.2), channel_id=1, source_target_pairs={{0,3},{1,2},{2,1},{3,0},{4,7},{5,6},{6,5},{7,4},{8,11},{9,10},{10,... | collective-permute-start | bytes 393224 | tf_op jit(solution)/shard_map/ppermute | solution.py:351
  16.4 4.0 %collective-permute-done.7.refs_5_ = f32[128,256]{1,0:T(8,128)S(1)} collective-permute-done((f32[128,256]{1,0:T(8,128)}, f32[128,256]{1,0:T(8,128)S(1)}, u32[]{:S(2)}, u32[]{:S(2)}) %collective-permute-start.7) | collective-permute-done | bytes 131104 | tf_op jit(solution)/shard_map/ppermute | solution.py:351
  20.4 3.4 %collective-permute-start.8 = (f32[128,256]{1,0:T(8,128)}, f32[128,256]{1,0:T(8,128)S(1)}, u32[]{:S(2)}, u32[]{:S(2)}) collective-permute-start(f32[128,256]{1,0:T(8,128)} %bitcast.3), channel_id=1, source_target_pairs={{0,2},{1,3},{2,0},{3,1},{4,6},{5,7},{6,4},{7,5},{8,10},{9,11},{10,... | collective-permute-start | bytes 393224 | tf_op jit(solution)/shard_map/ppermute | solution.py:351
  23.8 0.7 %collective-permute-start.9 = (f32[128,256]{1,0:T(8,128)}, f32[128,256]{1,0:T(8,128)S(1)}, u32[]{:S(2)}, u32[]{:S(2)}) collective-permute-start(f32[128,256]{1,0:T(8,128)} %bitcast.4), channel_id=1, source_target_pairs={{0,1},{1,0},{2,3},{3,2},{4,5},{5,4},{6,7},{7,6},{8,9},{9,8},{10,11... | collective-permute-start | bytes 393224 | tf_op jit(solution)/shard_map/ppermute | solution.py:351
  24.5 1.0 %shard_map.46 = (bf16[1536,256]{1,0:T(8,128)(2,1)S(1)}, f32[8,256]{1,0:T(8,128)S(1)}, bf16[512,1536]{1,0:T(8,128)(2,1)S(1)}, f32[16,256]{1,0:T(8,128)S(1)}, f32[2,16,256]{2,1,0:T(8,128)S(1)}) custom-call(f32[2,128]{1,0:T(2,128)S(1)} %get-tuple-element.17.inverse_ref, f32[136,256]{1,0:T(8,128)S(1)} %get-tuple-element.19.refs_0_.refs_4_, ...), custom_call_target="tpu_custom_call" | custom-call | tf_op jit(solution)/shard_map/pallas_call | solution.py:362
  25.5 3.4 %collective-permute-done.8.refs_4_ = f32[128,256]{1,0:T(8,128)S(1)} collective-permute-done((f32[128,256]{1,0:T(8,128)}, f32[128,256]{1,0:T(8,128)S(1)}, u32[]{:S(2)}, u32[]{:S(2)}) %collective-permute-start.8) | collective-permute-done | bytes 131104 | tf_op jit(solution)/shard_map/ppermute | solution.py:351
  28.9 0.7 %collective-permute-done.9.refs_5_ = f32[128,256]{1,0:T(8,128)S(1)} collective-permute-done((f32[128,256]{1,0:T(8,128)}, f32[128,256]{1,0:T(8,128)S(1)}, u32[]{:S(2)}, u32[]{:S(2)}) %collective-permute-start.9) | collective-permute-done | bytes 131104 | tf_op jit(solution)/shard_map/ppermute | solution.py:351
  29.7 0.9 %shard_map.47 = (bf16[1536,256]{1,0:T(8,128)(2,1)S(1)}, f32[8,256]{1,0:T(8,128)S(1)}, f32[16,512]{1,0:T(8,128)S(1)}, f32[2,16,512]{2,1,0:T(8,128)S(1)}) custom-call(f32[2,128]{1,0:T(2,128)S(1)} %get-tuple-element.17.inverse_ref, bf16[512,1536]{1,0:T(8,128)(2,1)S(1)} %get-tuple-element.22.stack, f32[16,256]{1,0:T(8,128)S(1)} %get-tuple-element.23.low_ref, ...), custom_call_target="tpu_custom_call" | custom-call | tf_op jit(solution)/shard_map/pallas_call | solution.py:362
  30.6 1.8 %shard_map.48.refs_0_ = f32[144,128]{1,0:T(8,128)S(1)} custom-call(f32[2,128]{1,0:T(2,128)S(1)} %get-tuple-element.17.inverse_ref, f32[64,32]{1,0:T(8,128)S(1)} %get-tuple-element.18.hot_ref, f32[8,256]{1,0:T(8,128)S(1)} %slice_add_fusion.picked_ref, bf16[1536,256]{1,0:T(8,128)(2,1)S(1)} %get-tuple-element.20.near_terms, ...), custom_call_target="tpu_custom_call" | custom-call | tf_op jit(solution)/shard_map/pallas_call | solution.py:362
  32.4 0.8 %collective-permute-start.10 = (f32[144,128]{1,0:T(8,128)S(1)}, f32[144,128]{1,0:T(8,128)S(1)}, u32[]{:S(2)}, u32[]{:S(2)}) collective-permute-start(f32[144,128]{1,0:T(8,128)S(1)} %shard_map.48.refs_0_), channel_id=1, source_target_pairs={{0,1},{1,0},{2,3},{3,2},{4,5},{5,4},{6,7},{7,6},{8,9},{9,8},{10,11... | collective-permute-start | bytes 221192 | tf_op jit(solution)/shard_map/ppermute | solution.py:351
  33.2 2.6 %collective-permute-start.11 = (f32[144,128]{1,0:T(8,128)S(1)}, f32[144,128]{1,0:T(8,128)S(1)}, u32[]{:S(2)}, u32[]{:S(2)}) collective-permute-start(f32[144,128]{1,0:T(8,128)S(1)} %shard_map.48.refs_0_), channel_id=1, source_target_pairs={{0,2},{1,3},{2,0},{3,1},{4,6},{5,7},{6,4},{7,5},{8,10},{9,11},{10,... | collective-permute-start | bytes 221192 | tf_op jit(solution)/shard_map/ppermute | solution.py:351
  35.8 1.0 %collective-permute-start.12 = (f32[144,128]{1,0:T(8,128)S(1)}, f32[144,128]{1,0:T(8,128)S(1)}, u32[]{:S(2)}, u32[]{:S(2)}) collective-permute-start(f32[144,128]{1,0:T(8,128)S(1)} %shard_map.48.refs_0_), channel_id=1, source_target_pairs={{0,3},{1,2},{2,1},{3,0},{4,7},{5,6},{6,5},{7,4},{8,11},{9,10},{10,... | collective-permute-start | bytes 221192 | tf_op jit(solution)/shard_map/ppermute | solution.py:351
  36.8 0.7 %collective-permute-done.10.refs_1_ = f32[144,128]{1,0:T(8,128)S(1)} collective-permute-done((f32[144,128]{1,0:T(8,128)S(1)}, f32[144,128]{1,0:T(8,128)S(1)}, u32[]{:S(2)}, u32[]{:S(2)}) %collective-permute-start.10) | collective-permute-done | bytes 73760 | tf_op jit(solution)/shard_map/ppermute | solution.py:351
  37.5 3.4 %collective-permute-done.11.refs_2_ = f32[144,128]{1,0:T(8,128)S(1)} collective-permute-done((f32[144,128]{1,0:T(8,128)S(1)}, f32[144,128]{1,0:T(8,128)S(1)}, u32[]{:S(2)}, u32[]{:S(2)}) %collective-permute-start.11) | collective-permute-done | bytes 73760 | tf_op jit(solution)/shard_map/ppermute | solution.py:351
  40.9 1.2 %collective-permute-done.12.refs_3_ = f32[144,128]{1,0:T(8,128)S(1)} collective-permute-done((f32[144,128]{1,0:T(8,128)S(1)}, f32[144,128]{1,0:T(8,128)S(1)}, u32[]{:S(2)}, u32[]{:S(2)}) %collective-permute-start.12) | collective-permute-done | bytes 73760 | tf_op jit(solution)/shard_map/ppermute | solution.py:351
  42.0 1.0 %shard_map.49 = f32[2,4,32]{2,1,0:T(4,128)} custom-call(f32[2,128]{1,0:T(2,128)S(1)} %get-tuple-element.17.inverse_ref, f32[144,128]{1,0:T(8,128)S(1)} %shard_map.48.refs_0_, f32[144,128]{1,0:T(8,128)S(1)} %collective-permute-done.10.refs_1_, f32[144,128]{1,0:T(8,128)S(1)} %collective-permute-done.11.refs_2_, f32[144,128]{1,0:T(8,128)S(1)} %collective-permute-done.12.refs_3_), custom_call_target="tpu_custom_call" | custom-call | tf_op jit(solution)/shard_map/pallas_call | solution.py:362
  (8 shorter events, 0.0 us)
Async XLA Ops:
  1.2 7.1 %collective-permute-start.1 = (f32[136,256]{1,0:T(8,128)S(1)}, f32[136,256]{1,0:T(8,128)S(1)}, u32[]{:S(2)}, u32[]{:S(2)}) collective-permute-start(f32[136,256]{1,0:T(8,128)S(1)} %get-tuple-element.19.refs_0_.refs_4_), channel_id=1, source_target_pairs={{0,8},{4,12},{8,0},{12,4},{16,24},{20,28},{24,16},{28,20},{1,9},{5... | collective-permute-start | bytes 417800 | tf_op jit(solution)/shard_map/ppermute | solution.py:351
  4.2 8.1 %collective-permute-start.3 = (f32[136,256]{1,0:T(8,128)S(1)}, f32[136,256]{1,0:T(8,128)S(1)}, u32[]{:S(2)}, u32[]{:S(2)}) collective-permute-start(f32[136,256]{1,0:T(8,128)S(1)} %get-tuple-element.19.refs_0_.refs_4_), channel_id=1, source_target_pairs={{0,16},{4,20},{8,24},{12,28},{16,0},{20,4},{24,8},{28,12},{1,17},{... | collective-permute-start | bytes 417800 | tf_op jit(solution)/shard_map/ppermute | solution.py:351
  5.7 6.6 %collective-permute-start.5 = (f32[136,256]{1,0:T(8,128)S(1)}, f32[136,256]{1,0:T(8,128)S(1)}, u32[]{:S(2)}, u32[]{:S(2)}) collective-permute-start(f32[136,256]{1,0:T(8,128)S(1)} %get-tuple-element.19.refs_0_.refs_4_), channel_id=1, source_target_pairs={{0,24},{4,28},{8,16},{12,20},{16,8},{20,12},{24,0},{28,4},{1,25},{... | collective-permute-start | bytes 417800 | tf_op jit(solution)/shard_map/ppermute | solution.py:351
  5.7 18.1 %collective-permute-start = (f32[136,256]{1,0:T(8,128)S(1)}, f32[136,256]{1,0:T(8,128)S(1)}, u32[]{:S(2)}, u32[]{:S(2)}) collective-permute-start(f32[136,256]{1,0:T(8,128)S(1)} %get-tuple-element.19.refs_0_.refs_4_), channel_id=1, source_target_pairs={{0,4},{4,0},{8,12},{12,8},{16,20},{20,16},{24,28},{28,24},{1,5},{5... | collective-permute-start | bytes 417800 | tf_op jit(solution)/shard_map/ppermute | solution.py:351
  8.2 16.3 %collective-permute-start.2 = (f32[136,256]{1,0:T(8,128)S(1)}, f32[136,256]{1,0:T(8,128)S(1)}, u32[]{:S(2)}, u32[]{:S(2)}) collective-permute-start(f32[136,256]{1,0:T(8,128)S(1)} %collective-permute-done.1.refs_2_), channel_id=1, source_target_pairs={{0,4},{4,0},{8,12},{12,8},{16,20},{20,16},{24,28},{28,24},{1,5},{5... | collective-permute-start | bytes 417800 | tf_op jit(solution)/shard_map/ppermute | solution.py:351
  12.3 13.2 %collective-permute-start.4 = (f32[136,256]{1,0:T(8,128)S(1)}, f32[136,256]{1,0:T(8,128)S(1)}, u32[]{:S(2)}, u32[]{:S(2)}) collective-permute-start(f32[136,256]{1,0:T(8,128)S(1)} %collective-permute-done.3.refs_0_), channel_id=1, source_target_pairs={{0,4},{4,0},{8,12},{12,8},{16,20},{20,16},{24,28},{28,24},{1,5},{5... | collective-permute-start | bytes 417800 | tf_op jit(solution)/shard_map/ppermute | solution.py:351
  12.3 13.2 %collective-permute-start.6 = (f32[136,256]{1,0:T(8,128)S(1)}, f32[136,256]{1,0:T(8,128)S(1)}, u32[]{:S(2)}, u32[]{:S(2)}) collective-permute-start(f32[136,256]{1,0:T(8,128)S(1)} %collective-permute-done.5.refs_2_), channel_id=1, source_target_pairs={{0,4},{4,0},{8,12},{12,8},{16,20},{20,16},{24,28},{28,24},{1,5},{5... | collective-permute-start | bytes 417800 | tf_op jit(solution)/shard_map/ppermute | solution.py:351
  12.8 7.6 %collective-permute-start.7 = (f32[128,256]{1,0:T(8,128)}, f32[128,256]{1,0:T(8,128)S(1)}, u32[]{:S(2)}, u32[]{:S(2)}) collective-permute-start(f32[128,256]{1,0:T(8,128)} %bitcast.2), channel_id=1, source_target_pairs={{0,3},{1,2},{2,1},{3,0},{4,7},{5,6},{6,5},{7,4},{8,11},{9,10},{10,... | collective-permute-start | bytes 393224 | tf_op jit(solution)/shard_map/ppermute | solution.py:351
  20.4 8.5 %collective-permute-start.8 = (f32[128,256]{1,0:T(8,128)}, f32[128,256]{1,0:T(8,128)S(1)}, u32[]{:S(2)}, u32[]{:S(2)}) collective-permute-start(f32[128,256]{1,0:T(8,128)} %bitcast.3), channel_id=1, source_target_pairs={{0,2},{1,3},{2,0},{3,1},{4,6},{5,7},{6,4},{7,5},{8,10},{9,11},{10,... | collective-permute-start | bytes 393224 | tf_op jit(solution)/shard_map/ppermute | solution.py:351
  23.8 5.8 %collective-permute-start.9 = (f32[128,256]{1,0:T(8,128)}, f32[128,256]{1,0:T(8,128)S(1)}, u32[]{:S(2)}, u32[]{:S(2)}) collective-permute-start(f32[128,256]{1,0:T(8,128)} %bitcast.4), channel_id=1, source_target_pairs={{0,1},{1,0},{2,3},{3,2},{4,5},{5,4},{6,7},{7,6},{8,9},{9,8},{10,11... | collective-permute-start | bytes 393224 | tf_op jit(solution)/shard_map/ppermute | solution.py:351
  32.4 5.2 %collective-permute-start.10 = (f32[144,128]{1,0:T(8,128)S(1)}, f32[144,128]{1,0:T(8,128)S(1)}, u32[]{:S(2)}, u32[]{:S(2)}) collective-permute-start(f32[144,128]{1,0:T(8,128)S(1)} %shard_map.48.refs_0_), channel_id=1, source_target_pairs={{0,1},{1,0},{2,3},{3,2},{4,5},{5,4},{6,7},{7,6},{8,9},{9,8},{10,11... | collective-permute-start | bytes 221192 | tf_op jit(solution)/shard_map/ppermute | solution.py:351
  33.2 7.7 %collective-permute-start.11 = (f32[144,128]{1,0:T(8,128)S(1)}, f32[144,128]{1,0:T(8,128)S(1)}, u32[]{:S(2)}, u32[]{:S(2)}) collective-permute-start(f32[144,128]{1,0:T(8,128)S(1)} %shard_map.48.refs_0_), channel_id=1, source_target_pairs={{0,2},{1,3},{2,0},{3,1},{4,6},{5,7},{6,4},{7,5},{8,10},{9,11},{10,... | collective-permute-start | bytes 221192 | tf_op jit(solution)/shard_map/ppermute | solution.py:351
  35.8 6.3 %collective-permute-start.12 = (f32[144,128]{1,0:T(8,128)S(1)}, f32[144,128]{1,0:T(8,128)S(1)}, u32[]{:S(2)}, u32[]{:S(2)}) collective-permute-start(f32[144,128]{1,0:T(8,128)S(1)} %shard_map.48.refs_0_), channel_id=1, source_target_pairs={{0,3},{1,2},{2,1},{3,0},{4,7},{5,6},{6,5},{7,4},{8,11},{9,10},{10,... | collective-permute-start | bytes 221192 | tf_op jit(solution)/shard_map/ppermute | solution.py:351
